TPU v7x, 128 devices: a whole 4x4x4 slice. The times are simulated.
128 devices in a mesh: gx: 16 (over y, z), gy: 8 (over x, core).
Axes of the slice: x: 4, y: 4, z: 4, core: 2. Of those that a mesh axis runs over, the one named last changes fastest.
Arguments:
- forces: float32 [3, 256, 256, 256], P(None, 'gx', 'gy'), may hold values from -8 to 8
- pressure_prev: float32 [256, 256, 256], P('gx', 'gy'), may hold values from -8 to 8
Outputs:
- pressure: float32 [256, 256, 256], P('gx', 'gy')
- residual: float32 [256, 256, 256], P('gx', 'gy')
All inputs are finite; a program needn't handle non-finite values.
Results may differ from a plain program's by a relative error of at most 0.0003.
Values sent between devices are 32-bit elements; how exact they have to be, the bound alone decides.
A program may use at most 64 MiB of HBM per device.

v0:
```python
import jax
import jax.numpy as jnp
from jax import lax
from jax.sharding import PartitionSpec as P

LEVELS = 5
COARSE_SWEEPS = 4
CYCLES = 2


OMEGA = 0.8


def extended(x, sides, width):
    edges = {}
    for axis, dim in sides:
        peers, length = (lax.axis_size(axis), x.shape[dim])
        up = [(i, (i + 1) % peers) for i in range(peers)]
        last = lax.slice_in_dim(x, length - width, length, axis=dim)
        initial = lax.slice_in_dim(x, 0, width, axis=dim)
        edges[dim] = (
            lax.ppermute(last, axis, up),
            lax.ppermute(initial, axis, [(b, a) for a, b in up]),
        )
    done = []
    for _, dim in sides:
        low, high = edges[dim]
        around = [(width, width) if d in done else (0, 0) for d in range(x.ndim)]
        x = jnp.concatenate([jnp.pad(low, around), x, jnp.pad(high, around)], axis=dim)
        done.append(dim)
    return x


def padded_2(x, sides, width):
    for axis, dim in sides:
        peers, length = (lax.axis_size(axis), x.shape[dim])
        up = [(i, (i + 1) % peers) for i in range(peers)]
        down = [(j, i) for i, j in up]
        last = lax.slice_in_dim(x, length - width, length, axis=dim)
        initial = lax.slice_in_dim(x, 0, width, axis=dim)
        before = lax.ppermute(last, axis, up)
        after = lax.ppermute(initial, axis, down)
        x = jnp.concatenate([before, x, after], axis=dim)
    return x


def laid_out(parts, dim):
    dims = list(parts.shape[1:])
    dims[dim] *= parts.shape[0]
    return jnp.moveaxis(parts, 0, dim).reshape(dims)


def sent_to_all(x, axis):
    copies = jnp.broadcast_to(x, (lax.axis_size(axis), *x.shape))
    return lax.all_to_all(copies, axis, split_axis=0, concat_axis=0, tiled=True)


def gather_directly(x, axis, dim):
    return laid_out(sent_to_all(x, axis), dim)


def shifted(block, axis, distance):
    devices = range(lax.axis_size(axis))
    route = [((i - distance) % len(devices), i) for i in devices]
    return lax.ppermute(block, axis, route)


def vertical(values):
    padded = jnp.pad(values, ((0, 0), (0, 0), (1, 1)))
    return padded[:, :, 2:] + padded[:, :, :-2]


def operate_padded(padded, weight):
    center = padded[1:-1, 1:-1]
    beside = padded[2:, 1:-1] + padded[:-2, 1:-1] + padded[1:-1, 2:] + padded[1:-1, :-2]
    return weight * (4.0 * center - beside) + (2.0 * center - vertical(center))


def relax(padded, source, weight):
    center = padded[1:-1, 1:-1]
    return center + OMEGA * (source - operate_padded(padded, weight)) / (4.0 * weight + 2.0)


def wrapped(values):
    return jnp.pad(values, ((1, 1), (1, 1), (0, 0)), mode="wrap")


def restrict(residual_now):
    rows_x, rows_y, depth = residual_now.shape
    return 0.25 * residual_now.reshape(rows_x // 2, 2, rows_y // 2, 2, depth).sum(axis=(1, 3))


def prolong(correction):
    return jnp.repeat(jnp.repeat(correction, 2, axis=0), 2, axis=1)


def mean_mode(values, source):
    depth = source.shape[2]
    column = jnp.mean(source, axis=(0, 1))
    lower = jnp.concatenate([jnp.zeros((1,), source.dtype), -jnp.ones((depth - 1,), source.dtype)])
    upper = jnp.concatenate([-jnp.ones((depth - 1,), source.dtype), jnp.zeros((1,), source.dtype)])
    middle = 2.0 * jnp.ones((depth,), source.dtype)
    profile = lax.linalg.tridiagonal_solve(lower, middle, upper, column[:, None])[:, 0]
    return values + profile[None, None, :]


def whole_cycle(values, source, level_index):
    weight = 0.25**level_index
    values = mean_mode(values, source)
    for sweep_index in range(COARSE_SWEEPS):
        values = relax(wrapped(values), source, weight)
    return values


def rimmed(values):
    return extended(values, (("gx", 0), ("gy", 1)), 1)


def smooth_local(values, source, weight):
    stacked = padded_2(jnp.stack([values, source]), (("gx", 1), ("gy", 2)), 2)
    widened = relax(stacked[0], stacked[1, 1:-1, 1:-1], weight)
    values = relax(widened, source, weight)
    return values


def local_cycle(values, source, level_index, gather_level):
    weight = 0.25**level_index
    if level_index == gather_level:
        gathered = gather_directly(source, "gy", 1)
        gathered = gather_directly(gathered, "gx", 0)
        solved = whole_cycle(jnp.zeros_like(gathered), gathered, level_index)
        start_x = lax.axis_index("gx") * source.shape[0]
        start_y = lax.axis_index("gy") * source.shape[1]
        return lax.dynamic_slice(solved, (start_x, start_y, jnp.int32(0)), source.shape)
    values = smooth_local(values, source, weight)
    residual_now = source - operate_padded(rimmed(values), weight)
    coarse_source = restrict(residual_now)
    correction = local_cycle(
        jnp.zeros_like(coarse_source), coarse_source, level_index + 1, gather_level
    )
    values = values + prolong(correction)
    return smooth_local(values, source, weight)


def on_device(forces, pressure_prev):
    force_x, force_y, force_z = (forces[0], forces[1], forces[2])
    from_left = shifted(force_x[-1:], "gx", 1)
    from_below = shifted(force_y[:, -1:], "gy", 1)
    behind_x = jnp.concatenate([from_left, force_x[:-1]], axis=0)
    behind_y = jnp.concatenate([from_below, force_y[:, :-1]], axis=1)
    behind_z = jnp.pad(force_z[:, :, :-1], ((0, 0), (0, 0), (1, 0)))
    source = behind_x - force_x + (behind_y - force_y) + (behind_z - force_z)
    gather_level = LEVELS - 1
    pressure = pressure_prev
    for cycle_index in range(CYCLES):
        pressure = local_cycle(pressure, source, 0, gather_level)
    residual = source - operate_padded(rimmed(pressure), 1.0)
    return (pressure, residual)


def solution(mesh):
    return jax.shard_map(
        on_device,
        mesh=mesh,
        in_specs=(P(None, "gx", "gy", None), P("gx", "gy", None)),
        out_specs=(P("gx", "gy", None), P("gx", "gy", None)),
        check_vma=False,
    )
```

profile of v0, /device:TPU:1, one launch (start us, length us, event | category | flops | bytes accessed | tf_op | source)
XLA Modules:
  0.0 1464.9 jit_solution(14959984055032230188)
XLA Ops:
  6.4 5.8 collective-permute-done
  13.4 4.8 collective-permute-start.3
  29.4 4.9 collective-permute-start.6
  55.3 5.1 collective-permute-start.14
  78.9 5.1 collective-permute-start.22
  90.1 4.8 collective-permute-start.27
  102.1 5.1 collective-permute-start.30
  114.7 10.8 all_to_all.20
  126.3 5.9 all-to-all-start.1
  132.2 7.4 all-to-all-done.1
  141.9 169.5 %while.64 = (s32[]{:T(128)}, f32[]{:T(128)}, f32[1]{0:T(128)}, f32[7,32]{1,0:T(8,128)S(1)}, f32[7,32,1]{1,2,0:T(1,128)S(1)}, /*index=5*/f32[7,32,1]{1,2,0:T(1,12...) while((s32[]{:T(128)}, f32[]{:T(128)}, f32[1]{0:T(128)}, f32[7,32]{1,0:T(8,128)S(1)}, ...), condition=%wide.region_7.8_spmd, body=%wide.region_6.7_spmd.sunk | while | flops 194 | bytes 4729 | solution.py:103
  337.3 302.1 %while.65 = (s32[]{:T(128)}, f32[1]{0:T(128)}, f32[7,32,1]{1,2,0:T(1,128)S(1)}, f32[7,32,1]{1,2,0:T(1,128)S(1)}, f32[7,32]{1,0:T(8,128)S(1)}, /*index=5*/s32[]{:T(128)}, s32[]{:T(128)}) while((s32[]{:T(128)}, f32[1]{0:T(128)}, f32[7,32,1]{1,2,0:T(1,128)S(1)}, f32[7,32,1]{1,2,0:T(1,128)S(1)}, f32[7,32]{1,0:T(8,128)S(1)}, /*index=5*/s32[]{:T(128)}, ...), condition=%wide.region_9.10_spmd, body=%wide.region_8.9_spmd.sunk | while | flops 67 | bytes 3173 | solution.py:103
  692.4 5.1 collective-permute-start.39
  703.6 4.9 collective-permute-start.43
  716.6 4.9 collective-permute-start.47
  731.4 5.3 collective-permute-start.51
  746.0 5.5 collective-permute-start.54
  760.5 4.8 collective-permute-start.59
  773.5 5.1 collective-permute-start.62
  786.5 4.8 collective-permute-start.67
  798.7 5.1 collective-permute-start.70
  811.4 4.8 collective-permute-start.75
  823.2 5.1 collective-permute-start.78
  835.8 10.8 all_to_all.21
  847.3 6.1 all-to-all-start.3
  853.4 7.4 all-to-all-done.3
  863.1 168.9 %while.66 = (s32[]{:T(128)}, f32[]{:T(128)}, f32[1]{0:T(128)}, f32[7,32]{1,0:T(8,128)S(1)}, f32[7,32,1]{1,2,0:T(1,128)S(1)}, /*index=5*/f32[7,32,1]{1,2,0:T(1,12...) while((s32[]{:T(128)}, f32[]{:T(128)}, f32[1]{0:T(128)}, ...), condition=%wide.region_17.18_spmd, body=%wide.region_16.17_spmd.sunk | while | flops 194 | bytes 4729 | solution.py:103
  1057.8 301.6 %while.67 = (s32[]{:T(128)}, f32[1]{0:T(128)}, f32[7,32,1]{1,2,0:T(1,128)S(1)}, f32[7,32,1]{1,2,0:T(1,128)S(1)}, f32[7,32]{1,0:T(8,128)S(1)}, /*index=5*/s32[]{:T(128)}, s32[]{:T(128)}) while((s32[]{:T(128)}, f32[1]{0:T(128)}, f32[7,32,1]{1,2,0:T(1,128)S(1)}, f32[7,32,1]{1,2,0:T(1,128)S(1)}, f32[7,32]{1,0:T(8,128)S(1)}, ...), condition=%wide.region_19.20_spmd, body=%wide.region_18.19_spmd.sunk | while | flops 67 | bytes 3173 | solution.py:103
  1412.4 5.1 collective-permute-start.87
  1423.6 4.9 collective-permute-start.91
  1436.6 4.9 collective-permute-start.95
  1451.3 4.9 collective-permute-start.98
  (702 shorter events, 305.7 us)
Async XLA Ops:
  4.7 7.5 collective-permute-start
  13.3 8.4 collective-permute-start.2
  13.4 8.3 collective-permute-start.3
  29.4 8.6 collective-permute-start.6
  41.5 6.5 collective-permute-start.10
  55.3 9.5 collective-permute-start.14
  78.9 11.0 collective-permute-start.22
  102.1 12.4 collective-permute-start.30
  107.3 7.3 collective-permute-start.31
  126.3 13.3 all-to-all-start.1
  703.5 6.6 collective-permute-start.42
  703.6 6.5 collective-permute-start.43
  716.5 7.3 collective-permute-start.46
  716.6 7.2 collective-permute-start.47
  731.3 7.3 collective-permute-start.50
  731.4 7.3 collective-permute-start.51
  746.0 13.3 collective-permute-start.54
  751.4 7.8 collective-permute-start.55
  760.4 6.5 collective-permute-start.58
  773.5 12.6 collective-permute-start.62
  778.6 7.5 collective-permute-start.63
  798.7 12.4 collective-permute-start.70
  803.8 7.3 collective-permute-start.71
  823.2 12.4 collective-permute-start.78
  828.4 7.2 collective-permute-start.79
  847.3 13.5 all-to-all-start.3
  1423.6 6.6 collective-permute-start.90
  1423.6 6.5 collective-permute-start.91
  1436.5 7.3 collective-permute-start.94
  1436.6 7.2 collective-permute-start.95
  1451.3 12.2 collective-permute-start.98
  1456.2 7.3 collective-permute-start.99
  (75 other events, 349.8 us)
where the time goes:
time: 1490 us; the launch traced here: 1460 us
  loops' own time  875 us (59%)
  starting transfers between devices  229 us (15%)
  between operations  125 us (8%)
  waiting for transfers between devices  112 us (8%)
  local copies, waits for them, and re-layouts  85.8 us (6%)
  blocking collectives  21.6 us (1%)
  other arithmetic  16.8 us (1%)
    another operation x4, loops' own time, mean_mode(): lax.linalg.tridiagonal_solve(lower, middle, upper, column[:, None])[:, 0]  875 us
    ppermute x32, starting transfers between devices, padded_2(): after = lax.ppermute(initial, axis, down)  105 us
    ppermute x18, starting transfers between devices, extended(): lax.ppermute(initial, axis, [(b, a) for a, b in up])  74 us
    slice x102, local copies, waits for them, and re-layouts, mean_mode(): lax.linalg.tridiagonal_solve(lower, middle, upper, column[:, None])[:, 0]  69.6 us
    ppermute x32, waiting for transfers between devices, padded_2(): before = lax.ppermute(last, axis, up)  38.6 us
    ppermute x32, starting transfers between devices, padded_2(): before = lax.ppermute(last, axis, up)  31.5 us
  transfers between devices with their start and end apart: 104, of which 72 were waited for; matrix products, arithmetic and copies ran while one was open for 0% of the time, Pallas kernels for 0%

commit v1 on v0

v1 whole, which is shorter than its diff:
```python
import functools

import jax
import jax.numpy as jnp
import numpy as np
from jax import lax
from jax.experimental import pallas as pl
from jax.experimental.pallas import tpu as pltpu
from jax.sharding import PartitionSpec as P

MESH = pl.DeviceIdType.MESH
OMEGA = 0.8
LEVELS = 5
GX, GY = 16, 8
NDEV = GX * GY
BX, BY, NZ = 16, 32, 256
HIGHEST = lax.Precision.HIGHEST


def sine_matrix(weight=1.0):
    k = np.arange(1, NZ + 1, dtype=np.float64)
    return (weight * (np.sqrt(2.0 / (NZ + 1)) * np.sin(np.pi * np.outer(k, k) / (NZ + 1)))).astype(np.float32)


def spectrum():
    k = np.arange(1, NZ + 1, dtype=np.float64)
    return 4.0 * np.sin(0.5 * np.pi * k / (NZ + 1)) ** 2


def eigenvalues():
    rows = np.tile(spectrum().reshape(NDEV, 2), (1, 4))
    return np.broadcast_to(rows[:, :, None], (NDEV, 8, 128)).astype(np.float32)


def iota(axis):
    return lax.broadcasted_iota(jnp.int32, (8, 128), axis)


def exchange_blocks(vectors, axis, unit):
    size = 4 * unit
    place = iota(axis) // unit
    low, even = place < 2, lax.rem(place, 2) == 0
    a = list(vectors)
    for i in (0, 1):
        x, y = a[i], a[i + 2]
        a[i] = jnp.where(low, x, pltpu.roll(y, 2 * unit, axis))
        a[i + 2] = jnp.where(low, pltpu.roll(x, 2 * unit, axis), y)
    for i in (0, 2):
        x, y = a[i], a[i + 1]
        a[i] = jnp.where(even, x, pltpu.roll(y, unit, axis))
        a[i + 1] = jnp.where(even, pltpu.roll(x, size - unit, axis), y)
    return a


def remap(grid):
    cols = [exchange_blocks([grid[q][g] for q in range(4)], 0, 2) for g in range(4)]
    return [exchange_blocks([cols[g][t] for g in range(4)], 1, 32) for t in range(4)]


def remap_back(grid):
    rows = [exchange_blocks(grid[t], 1, 32) for t in range(4)]
    cols = [exchange_blocks([rows[t][g] for t in range(4)], 0, 2) for g in range(4)]
    return [[cols[g][q] for g in range(4)] for q in range(4)]


class Plane:
    def __init__(self, ref, n):
        self.ref, self.n = ref, n

    def get(self, i, h):
        if i < 0:
            return pltpu.roll(self.ref[self.n - 1, h], 2, 0)
        if i >= self.n:
            return pltpu.roll(self.ref[0, h], 6, 0)
        return self.ref[i, h]

    def put(self, i, h, value):
        self.ref[i, h] = value


def neighbours(v, i, h, step, lane):
    own, other = v.get(i, h), v.get(i, 1 - h)
    below = pltpu.roll(jnp.where(lane >= 128 - step, other, own), step, 1)
    above = pltpu.roll(jnp.where(lane < step, other, own), 128 - step, 1)
    return (v.get(i - 1, h) + v.get(i + 1, h)) + (below + above)


def shifted_rows(a, edge, up):
    rows = a.shape[0]
    row = lax.broadcasted_iota(jnp.int32, a.shape, 0)
    if up:
        return jnp.where(row == rows - 1, edge, pltpu.roll(a, rows - 1, 0))
    return jnp.where(row == 0, edge, pltpu.roll(a, 1, 0))


def shifted_depth(a, up):
    depth = a.shape[1]
    col = lax.broadcasted_iota(jnp.int32, a.shape, 1)
    if up:
        return jnp.where(col == depth - 1, 0.0, pltpu.roll(a, depth - 1, 1))
    return jnp.where(col == 0, 0.0, pltpu.roll(a, 1, 1))


def transform(x, y, dim):
    return lax.dot_general(x, y, (((dim,), (dim,)), ((), ())), precision=HIGHEST, preferred_element_type=jnp.float32)


def coords(i):
    return (i // GY, lax.rem(i, GY))


def kernel(
    f_ref, p_ref, s_ref, st_ref, lam_hbm,
    pressure_ref, residual_ref,
    lam_ref, r_ref, o_ref, send, recv, back, e_ref, send_x, send_y, halo_x, halo_y,
    f0, f1, f2, f3, f4, a0, a1, a2, a3, a4, b0, b1, b2, b3, b4,
    lam_sem, hs_sem, hr_sem, s_sem, r_sem,
):
    gx, gy = lax.axis_index("gx"), lax.axis_index("gy")
    me = gx * GY + gy
    barrier = pltpu.get_barrier_semaphore()

    def greet(k, c):
        pl.semaphore_signal(barrier, inc=1, device_id=coords(lax.rem(me + k, NDEV)), device_id_type=MESH)
        return c

    lax.fori_loop(1, NDEV, greet, 0)
    lam_copy = pltpu.make_async_copy(lam_hbm.at[me], lam_ref, lam_sem)
    lam_copy.start()

    right, left = (lax.rem(gx + 1, GX), gy), (lax.rem(gx + GX - 1, GX), gy)
    upper, lower = (gx, lax.rem(gy + 1, GY)), (gx, lax.rem(gy + GY - 1, GY))

    def edge_copies(round_index):
        plan = ((send_x, halo_x, 0, right), (send_x, halo_x, 1, left), (send_y, halo_y, 0, upper), (send_y, halo_y, 1, lower))
        return [
            pltpu.make_async_remote_copy(
                source.at[round_index, side], target.at[round_index, side],
                hs_sem.at[round_index, n], hr_sem.at[round_index, n], device_id=to, device_id_type=MESH,
            )
            for n, (source, target, side, to) in enumerate(plan)
        ]

    send_x[0, 0] = f_ref[0, BX - 1] + p_ref[BX - 1]
    send_x[0, 1] = p_ref[0]
    for i in range(BX):
        send_y[0, 0, i] = f_ref[1, i, BY - 1] + p_ref[i, BY - 1]
        send_y[0, 1, i] = p_ref[i, 0]

    for i in range(BX):
        p, fx, fy, fz = p_ref[i], f_ref[0, i], f_ref[1, i], f_ref[2, i]
        r = shifted_depth(fz, False) - ((fx + fy + fz) + 4.0 * p)
        r = r + (shifted_rows(fy + p, 0.0, False) + shifted_rows(p, 0.0, True))
        if i > 0:
            r = r + (f_ref[0, i - 1] + p_ref[i - 1])
        if i < BX - 1:
            r = r + p_ref[i + 1]
        r_ref[i] = r

    pl.semaphore_wait(barrier, NDEV - 1)
    copies = edge_copies(0)
    for copy in copies:
        copy.start()
    for copy in copies:
        copy.wait()
    r_ref[0] = r_ref[0] + halo_x[0, 0]
    r_ref[BX - 1] = r_ref[BX - 1] + halo_x[0, 1]
    for i in range(BX):
        r_ref[i, 0] = r_ref[i, 0] + halo_y[0, 0, i]
        r_ref[i, BY - 1] = r_ref[i, BY - 1] + halo_y[0, 1, i]

    for t in range(4):
        rows = r_ref[4 * t : 4 * t + 4].reshape(128, NZ)
        flat = p_ref[4 * t : 4 * t + 4].reshape(128, NZ)
        o_ref[t] = transform(s_ref[...], rows, 1) + transform(st_ref[...], flat, 1)
    for g in range(32):
        parts = exchange_blocks([o_ref[t, 8 * g : 8 * g + 8] for t in range(4)], 0, 2)
        for j in range(4):
            send[4 * g + j] = parts[j]

    def all_to_all(target, which):
        def start(k, c):
            to = lax.rem(me + k, NDEV)
            pltpu.make_async_remote_copy(
                send.at[to], target.at[me], s_sem.at[which], r_sem.at[which], device_id=coords(to), device_id_type=MESH
            ).start()
            return c

        lax.fori_loop(1, NDEV, start, 0)
        target[me] = send[me]
        most = target.at[pl.ds(0, NDEV - 1)]
        pltpu.make_async_copy(most, most, r_sem.at[which]).wait()
        pltpu.make_async_copy(most, most, s_sem.at[which]).wait()

    all_to_all(recv, 0)
    lam_copy.wait()

    for gl in range(4):
        for h in range(2):
            grid = [[recv[(4 * q + gl) * GY + 4 * h + g] for g in range(4)] for q in range(4)]
            grid = remap(grid)
            for t in range(4):
                for x in range(4):
                    f0[16 * gl + 4 * t + x, h] = grid[t][x]

    lane = iota(1)
    lam = lam_ref[...]
    sizes = [64 >> level for level in range(LEVELS)]
    f = [Plane(ref, n) for ref, n in zip((f0, f1, f2, f3, f4), sizes)]
    a = [Plane(ref, n) for ref, n in zip((a0, a1, a2, a3, a4), sizes)]
    b = [Plane(ref, n) for ref, n in zip((b0, b1, b2, b3, b4), sizes)]

    def every(n):
        return ((i, h) for i in range(n) for h in range(2))

    def sweep(level, source, target):
        w = 0.25**level
        c = OMEGA / (4.0 * w + 2.0)
        keep = 1.0 - c * (4.0 * w + lam)
        for i, h in every(sizes[level]):
            beside = neighbours(source, i, h, 1 << level, lane)
            target.put(i, h, keep * source.get(i, h) + ((c * w) * beside + c * f[level].get(i, h)))

    def first_two(level, target):
        w = 0.25**level
        c = OMEGA / (4.0 * w + 2.0)
        keep = c * (2.0 - c * (4.0 * w + lam))
        for i, h in every(sizes[level]):
            beside = neighbours(f[level], i, h, 1 << level, lane)
            target.put(i, h, keep * f[level].get(i, h) + (c * c * w) * beside)

    def coarsen(level, source):
        w, step = 0.25**level, 1 << level
        first = lax.rem(lane // step, 2) == 0

        def rest(i, h):
            beside = neighbours(source, i, h, step, lane)
            own = source.get(i, h)
            return f[level].get(i, h) - (w * (4.0 * own - beside) + lam * own)

        for i, h in every(sizes[level + 1]):
            both = rest(2 * i, h) + rest(2 * i + 1, h)
            partner = jnp.where(first, pltpu.roll(both, 128 - step, 1), pltpu.roll(both, step, 1))
            f[level + 1].put(i, h, 0.25 * (both + partner))

    def correct(level, target, e):
        for i, h in every(sizes[level]):
            target.put(i, h, target.get(i, h) + e.get(i // 2, h))

    def coarsest(level):
        w = 0.25**level
        c = OMEGA / (4.0 * w + 2.0)
        total = functools.reduce(jnp.add, [f[level].get(i, h) for i, h in every(sizes[level])])
        total = total + pltpu.roll(total, 4, 0)
        total = total + pltpu.roll(total, 2, 0)
        mean = jnp.sum(total, axis=1, keepdims=True) * (1.0 / (2 * 4 * sizes[level] * 128))
        u = jnp.broadcast_to(mean, (8, 128)) / lam
        start = (1.0 - c * lam) * u
        for i, h in every(sizes[level]):
            a[level].put(i, h, start + c * f[level].get(i, h))
        sweep(level, a[level], b[level])
        sweep(level, b[level], a[level])
        sweep(level, a[level], b[level])
        return b[level]

    def cycle(level, first):
        if level == LEVELS - 1:
            return coarsest(level)
        if first:
            first_two(level, b[level])
        else:
            sweep(level, b[level], a[level])
            sweep(level, a[level], b[level])
        coarsen(level, b[level])
        e = cycle(level + 1, True)
        correct(level, b[level], e)
        sweep(level, b[level], a[level])
        sweep(level, a[level], b[level])
        return b[level]

    cycle(0, True)
    cycle(0, False)

    for gl in range(4):
        for h in range(2):
            grid = [[b0[16 * gl + 4 * t + x, h] for x in range(4)] for t in range(4)]
            grid = remap_back(grid)
            for q in range(4):
                for g in range(4):
                    send[(4 * q + gl) * GY + 4 * h + g] = grid[q][g]

    all_to_all(back, 1)

    for g in range(32):
        parts = exchange_blocks([back[4 * g + j] for j in range(4)], 0, 2)
        for t in range(4):
            o_ref[t, 8 * g : 8 * g + 8] = parts[t]
    for t in range(4):
        rows = transform(o_ref[t], s_ref[...], 0)
        e_ref[4 * t : 4 * t + 4] = rows.reshape(4, BY, NZ)

    send_x[1, 0] = e_ref[BX - 1]
    send_x[1, 1] = e_ref[0]
    for i in range(BX):
        send_y[1, 0, i] = e_ref[i, BY - 1]
        send_y[1, 1, i] = e_ref[i, 0]
    copies = edge_copies(1)
    for copy in copies:
        copy.start()
    for i in range(BX):
        e = e_ref[i]
        p = p_ref[i] + e
        pressure_ref[i] = p
        r = r_ref[i] - 4.0 * e + (shifted_depth(p, False) + shifted_depth(p, True) - 2.0 * p)
        r = r + (shifted_rows(e, 0.0, False) + shifted_rows(e, 0.0, True))
        if i > 0:
            r = r + e_ref[i - 1]
        if i < BX - 1:
            r = r + e_ref[i + 1]
        residual_ref[i] = r
    for copy in copies:
        copy.wait()
    residual_ref[0] = residual_ref[0] + halo_x[1, 0]
    residual_ref[BX - 1] = residual_ref[BX - 1] + halo_x[1, 1]
    for i in range(BX):
        residual_ref[i, 0] = residual_ref[i, 0] + halo_y[1, 0, i]
        residual_ref[i, BY - 1] = residual_ref[i, BY - 1] + halo_y[1, 1, i]


def on_device(forces, pressure_prev):
    block = (BX, BY, NZ)
    vmem = pl.BlockSpec(memory_space=pltpu.VMEM)
    levels = [pltpu.VMEM((64 >> level, 2, 8, 128), jnp.float32) for level in range(LEVELS)]
    return pl.pallas_call(
        kernel,
        out_shape=(jax.ShapeDtypeStruct(block, jnp.float32), jax.ShapeDtypeStruct(block, jnp.float32)),
        in_specs=[vmem, vmem, vmem, vmem, pl.BlockSpec(memory_space=pl.ANY)],
        out_specs=(vmem, vmem),
        scratch_shapes=[
            pltpu.VMEM((8, 128), jnp.float32),
            pltpu.VMEM(block, jnp.float32),
            pltpu.VMEM((4, NZ, 128), jnp.float32),
            pltpu.VMEM((NDEV, 8, 128), jnp.float32),
            pltpu.VMEM((NDEV, 8, 128), jnp.float32),
            pltpu.VMEM((NDEV, 8, 128), jnp.float32),
            pltpu.VMEM(block, jnp.float32),
            pltpu.VMEM((2, 2, BY, NZ), jnp.float32),
            pltpu.VMEM((2, 2, BX, NZ), jnp.float32),
            pltpu.VMEM((2, 2, BY, NZ), jnp.float32),
            pltpu.VMEM((2, 2, BX, NZ), jnp.float32),
            *levels, *levels, *levels,
            pltpu.SemaphoreType.DMA,
            pltpu.SemaphoreType.DMA((2, 4)),
            pltpu.SemaphoreType.DMA((2, 4)),
            pltpu.SemaphoreType.DMA((2,)),
            pltpu.SemaphoreType.DMA((2,)),
        ],
        compiler_params=pltpu.CompilerParams(collective_id=0, has_side_effects=True),
        name="poisson",
    )(
        forces,
        pressure_prev,
        jnp.asarray(sine_matrix()),
        jnp.asarray(sine_matrix(-spectrum()[:, None])),
        jnp.asarray(eigenvalues()),
    )


def solution(mesh):
    return jax.shard_map(
        on_device,
        mesh=mesh,
        in_specs=(P(None, "gx", "gy", None), P("gx", "gy", None)),
        out_specs=(P("gx", "gy", None), P("gx", "gy", None)),
        check_vma=False,
    )
```

time: 1490 us -> 75.7 us (0.05); the launches traced: 1460 us -> 75.5 us
  loops' own time: 875 us -> 0 us
  starting transfers between devices: 229 us -> 0 us
  between operations: 125 us -> 0.64 us
  waiting for transfers between devices: 112 us -> 0 us
  local copies, waits for them, and re-layouts: 85.8 us -> 3.76 us
  Pallas kernels: 0 us -> 71.1 us
  blocking collectives: 21.6 us -> 0 us
  other arithmetic: 16.8 us -> 0 us
    another operation x4 -> x0, loops' own time: 875 us -> none  [mean_mode(): lax.linalg.tridiagonal_solve(lower, middle, upper, column[:, None])[:, 0]]
    ppermute x102 -> x0, starting transfers between devices: 217 us -> none  [the longest x32 105 us: padded_2(): after = lax.ppermute(initial, axis, down)]
    ppermute x102 -> x0, waiting for transfers between devices: 97.3 us -> none  [the longest x32 38.6 us: padded_2(): before = lax.ppermute(last, axis, up)]
    pallas_call x0 -> x1, Pallas kernels: none -> 71.1 us  [on_device(): pl.pallas_call(kernel, out_shape=(jax.ShapeDtypeStruct(block, jnp.float32...]
    slice x175 -> x0, local copies, waits for them, and re-layouts: 70.9 us -> none  [the longest x102 69.6 us: mean_mode(): lax.linalg.tridiagonal_solve(lower, middle, upper, column[:, None])[:, 0]]
    all_to_all x2 -> x0, blocking collectives: 21.6 us -> none  [sent_to_all(): return lax.all_to_all(copies, axis, split_axis=0, concat_axis=0, tiled=True)]
  transfers between devices with their start and end apart: 104 -> 0, of which waited for: 72 -> 0; matrix products, arithmetic and copies ran while one was open for 0% -> 0% of each run, Pallas kernels for 0% -> 0%
where the time goes in v1:
time: 75.7 us; the launch traced here: 75.5 us
  Pallas kernels  71.1 us (94%)
  local copies, waits for them, and re-layouts  3.76 us (5%)
    pallas_call x1, Pallas kernels, on_device(): pl.pallas_call(kernel, out_shape=(jax.ShapeDtypeStruct(block, jnp.float32...  71.1 us
    unnamed x2, local copies, waits for them, and re-layouts  3.76 us

profile of v1, /device:TPU:1, one launch (start us, length us, event | category | flops | bytes accessed | tf_op | source)
XLA Modules:
  0.0 75.5 jit_solution(7349740057034102876)
XLA Ops:
  0.6 71.1 %poisson.1 = (f32[16,32,256]{2,1,0:T(8,128)}, f32[16,32,256]{2,1,0:T(8,128)}) custom-call(f32[3,16,32,256]{3,2,1,0:T(8,128)} %f_ref.1, f32[16,32,256]{2,1,0:T(8,128)} %p_ref.1, f32[256,256]{1,0:T(8,128)} %constant.6.clone.s_ref, f32[256,256]{1,0:T(8,128)} %constant.7.clone.st_ref, f32[128,8,128]{2,1,0:T(8,128)} %constant.8.clone.lam_hbm), custom_call_target="tpu_custom_call" | custom-call | tf_op jit(solution)/shard_map/poisson/pallas_call | solution.py:334
  71.7 1.9 %copy.9 = f32[16,32,256]{2,1,0:T(8,128)} copy(f32[16,32,256]{2,1,0:T(8,128)} %get-tuple-element.4) | data formatting | bytes 1048576
  73.6 1.9 %copy.10 = f32[16,32,256]{2,1,0:T(8,128)} copy(f32[16,32,256]{2,1,0:T(8,128)} %get-tuple-element.5) | data formatting | bytes 1048576

commit v2 on v0

v2 whole, which is shorter than its diff:
```python
import contextlib
import functools

import jax
import jax.numpy as jnp
import numpy as np
from jax import lax
from jax.experimental import pallas as pl
from jax.experimental.pallas import tpu as pltpu
from jax.sharding import PartitionSpec as P

MESH = pl.DeviceIdType.MESH
OMEGA = 0.8
LEVELS = 5
GX, GY = 16, 8
NDEV = GX * GY
BX, BY, NZ = 16, 32, 256
TILES = 5
ROWS = 2 * TILES
HIGHEST = lax.Precision.HIGHEST
SCOPES = False


def scope(name):
    return jax.named_scope(name) if SCOPES else contextlib.nullcontext()


def spectrum():
    k = np.arange(1, NZ + 1, dtype=np.float64)
    return 4.0 * np.sin(0.5 * np.pi * k / (NZ + 1)) ** 2


def sine_matrix(weight=1.0):
    k = np.arange(1, NZ + 1, dtype=np.float64)
    return (weight * (np.sqrt(2.0 / (NZ + 1)) * np.sin(np.pi * np.outer(k, k) / (NZ + 1)))).astype(np.float32)


def eigenvalues():
    rows = np.tile(spectrum().reshape(NDEV, 2), (1, 4))
    return np.broadcast_to(rows[:, :, None], (NDEV, 8, 128)).astype(np.float32)


def iota(axis):
    return lax.broadcasted_iota(jnp.int32, (8, 128), axis)


def shifted_rows(a, up):
    rows = a.shape[0]
    row = lax.broadcasted_iota(jnp.int32, a.shape, 0)
    if up:
        return jnp.where(row == rows - 1, 0.0, pltpu.roll(a, rows - 1, 0))
    return jnp.where(row == 0, 0.0, pltpu.roll(a, 1, 0))


def shifted_depth(a, up):
    depth = a.shape[1]
    col = lax.broadcasted_iota(jnp.int32, a.shape, 1)
    if up:
        return jnp.where(col == depth - 1, 0.0, pltpu.roll(a, depth - 1, 1))
    return jnp.where(col == 0, 0.0, pltpu.roll(a, 1, 1))


def transform(x, y, dim):
    return lax.dot_general(x, y, (((dim,), (dim,)), ((), ())), precision=HIGHEST, preferred_element_type=jnp.float32)


def fence():
    pl.delay(1)


class Lanes:
    def __init__(self):
        gx = lax.rem(iota(1), GX)
        self.first, self.last = gx == 0, gx == GX - 1
        self.sub = iota(0)

    def from_left(self, v):
        return jnp.where(self.first, pltpu.roll(v, 128 - (GX - 1), 1), pltpu.roll(v, 1, 1))

    def from_right(self, v):
        return jnp.where(self.last, pltpu.roll(v, GX - 1, 1), pltpu.roll(v, 127, 1))

    def from_below(self, v):
        return pltpu.roll(v, GX, 1)

    def from_above(self, v):
        return pltpu.roll(v, 128 - GX, 1)


class Field:
    def __init__(self, level, ref=None):
        self.level, self.ref, self.held = level, ref, {}
        self.nx, self.ny = BX >> level, max(1, 4 >> level)
        self.step = max(1, (1 << level) // 4)

    def cells(self):
        return [(x, y) for x in range(self.nx) for y in range(self.ny)]

    def get(self, x, y):
        return self.held[x, y] if self.ref is None else self.ref[x, y]

    def put(self, x, y, value):
        if self.ref is None:
            self.held[x, y] = value
        else:
            self.ref[x, y] = value

    def beside(self, x, y, lanes):
        step = self.step
        left = self.get(x - 1, y) if x > 0 else lanes.from_left(self.get(self.nx - 1, y))
        right = self.get(x + 1, y) if x < self.nx - 1 else lanes.from_right(self.get(0, y))
        if y > 0:
            below = self.get(x, y - 1)
        else:
            below = pltpu.roll(self.get(x, self.ny - 1), step, 0)
            below = jnp.where(lanes.sub < step, lanes.from_below(below), below)
        if y < self.ny - 1:
            above = self.get(x, y + 1)
        else:
            above = pltpu.roll(self.get(x, 0), 8 - step, 0)
            above = jnp.where(lanes.sub >= 8 - step, lanes.from_above(above), above)
        return (left + right) + (below + above)


def weights(level):
    w = 0.25**level
    return w, OMEGA / (4.0 * w + 2.0)


def sweep(source, f, target, lam, lanes):
    w, c = weights(source.level)
    keep = 1.0 - c * (4.0 * w + lam)
    for x, y in source.cells():
        beside = source.beside(x, y, lanes)
        target.put(x, y, keep * source.get(x, y) + ((c * w) * beside + c * f.get(x, y)))


def first_two(f, target, lam, lanes):
    w, c = weights(f.level)
    keep = c * (2.0 - c * (4.0 * w + lam))
    for x, y in f.cells():
        target.put(x, y, keep * f.get(x, y) + (c * c * w) * f.beside(x, y, lanes))


def coarsen(source, f, coarse, lam, lanes):
    w, _ = weights(source.level)

    def rest(x, y):
        own = source.get(x, y)
        return f.get(x, y) - (w * (4.0 * own - source.beside(x, y, lanes)) + lam * own)

    for x, y in coarse.cells():
        if source.ny > 1:
            total = (rest(2 * x, 2 * y) + rest(2 * x + 1, 2 * y)) + (rest(2 * x, 2 * y + 1) + rest(2 * x + 1, 2 * y + 1))
        else:
            step = source.step
            both = rest(2 * x, y) + rest(2 * x + 1, y)
            even = lax.rem(lanes.sub // step, 2) == 0
            total = both + jnp.where(even, pltpu.roll(both, 8 - step, 0), pltpu.roll(both, step, 0))
        coarse.put(x, y, 0.25 * total)


def correct(target, e):
    for x, y in target.cells():
        target.put(x, y, target.get(x, y) + e.get(x // 2, y // 2 if target.ny > 1 else 0))


def coarsest(f, lam, lanes):
    level = f.level
    _, c = weights(level)
    own = f.get(0, 0)
    total = jnp.broadcast_to(jnp.sum(own, axis=1, keepdims=True), (8, 128))
    total = total + pltpu.roll(total, 4, 0)
    total = total + pltpu.roll(total, 2, 0)
    total = total + pltpu.roll(total, 1, 0)
    u = (total * (1.0 / 1024.0)) / lam
    v = Field(level)
    v.put(0, 0, (1.0 - c * lam) * u + c * own)
    for _ in range(3):
        new = Field(level)
        sweep(v, f, new, lam, lanes)
        v = new
    return v


def kernel(
    f_hbm, p_hbm, s_hbm, st_hbm, lam_hbm,
    pressure_hbm, residual_hbm,
    f_ref, p_ref, s_ref, st_ref, lam_ref, r_ref, g_ref, o_ref, e_ref, ends_ref, pressure_ref, residual_ref,
    send, recv, reply, back, w_ref, row_ref, f0, a0, b0, f1, a1, b1,
    in_sem, out_sem, s_sem, r_sem,
):
    gx, gy = lax.axis_index("gx"), lax.axis_index("gy")
    me = gy * GX + gx
    loads = [
        pltpu.make_async_copy(source, target, in_sem.at[n])
        for n, (source, target) in enumerate(
            ((f_hbm, f_ref), (p_hbm, p_ref), (s_hbm, s_ref), (st_hbm, st_ref), (lam_hbm.at[me], lam_ref))
        )
    ]
    for load in loads:
        load.start()

    to_x = [lax.rem(gx + a, GX) for a in range(GX)]

    def partners(visit):
        for a in range(1, GX):
            visit(to_x[a], gy)

        def row(b, c):
            y = lax.rem(gy + b, GY)
            for a in range(GX):
                visit(to_x[a], y)
            return c

        lax.fori_loop(1, GY, row, 0)

    barrier = pltpu.get_barrier_semaphore()
    with scope("greet"):
        partners(lambda x, y: pl.semaphore_signal(barrier, inc=1, device_id=(x, y), device_id_type=MESH))
    with scope("load"):
        for load in loads:
            load.wait()

    with scope("stage_a"):
        g_ref[0:32] = f_ref[0, BX - 1] + p_ref[BX - 1]
        g_ref[32:64] = p_ref[0]
        g_ref[96:128] = jnp.zeros((32, NZ), jnp.float32)
        for i in range(BX):
            p, fx, fy, fz = p_ref[i], f_ref[0, i], f_ref[1, i], f_ref[2, i]
            r = shifted_depth(fz, False) - ((fx + fy + fz) + 4.0 * p)
            r = r + (shifted_rows(fy + p, False) + shifted_rows(p, True))
            if i > 0:
                r = r + (f_ref[0, i - 1] + p_ref[i - 1])
            if i < BX - 1:
                r = r + p_ref[i + 1]
            r_ref[i] = r
            g_ref[64 + i] = f_ref[1, i, BY - 1] + p_ref[i, BY - 1]
            g_ref[80 + i] = p_ref[i, 0]

    with scope("dst"):
        for t in range(4):
            rows = r_ref[4 * t : 4 * t + 4].reshape(128, NZ)
            flat = p_ref[4 * t : 4 * t + 4].reshape(128, NZ)
            o_ref[t] = transform(s_ref[...], rows, 1) + transform(st_ref[...], flat, 1)
        o_ref[4] = transform(s_ref[...], g_ref[...], 1)
    with scope("pack"):
        for t in range(TILES):
            for k in range(2):
                send[pl.ds(2 * t + k, NDEV, stride=ROWS), :] = o_ref[t, pl.ds(k, NDEV, stride=2), :]

    with scope("barrier"):
        pl.semaphore_wait(barrier, NDEV - 1)

    def blocks(ref, index):
        return ref.at[pl.ds(index * ROWS, ROWS)]

    def start_all_to_all(source, target, which):
        mine = blocks(target, me)

        def visit(x, y):
            pltpu.make_async_remote_copy(
                blocks(source, y * GX + x), mine, s_sem.at[which], r_sem.at[which], device_id=(x, y), device_id_type=MESH
            ).start()

        partners(visit)
        target[pl.ds(me * ROWS, ROWS), :] = source[pl.ds(me * ROWS, ROWS), :]

    def wait_all(ref, sem):
        most = ref.at[pl.ds(0, (NDEV - 1) * ROWS)]
        pltpu.make_async_copy(most, most, sem).wait()

    with scope("a2a_1_start"):
        start_all_to_all(send, recv, 0)
    with scope("a2a_1_wait"):
        wait_all(recv, r_sem.at[0])

    lanes = Lanes()
    with scope("unpack"):
        for n in range(ROWS):
            w_ref[n] = recv[pl.ds(n, NDEV, stride=ROWS), :].T
        for k in range(2):
            for half in range(2):
                at = 8 * half
                row_ref[k, at : at + 8] = lanes.from_below(w_ref[8 + k, 64 + at : 72 + at])
                row_ref[k, 16 + at : 24 + at] = lanes.from_above(w_ref[8 + k, 80 + at : 88 + at])
        for k in range(2):
            for x in range(BX):
                t, x4 = divmod(x, 4)
                for y in range(4):
                    value = w_ref[2 * t + k, pl.ds(32 * x4 + y, 8, stride=4), :]
                    if x == 0:
                        value = value + lanes.from_left(w_ref[8 + k, pl.ds(y, 8, stride=4), :])
                    if x == BX - 1:
                        value = value + lanes.from_right(w_ref[8 + k, pl.ds(32 + y, 8, stride=4), :])
                    if y == 0:
                        value = value + jnp.where(lanes.sub == 0, row_ref[k, x : x + 1], 0.0)
                    if y == 3:
                        value = value + jnp.where(lanes.sub == 7, row_ref[k, 16 + x : 17 + x], 0.0)
                    f0[k, x, y] = value

    lams = [jnp.broadcast_to(lam_ref[k : k + 1], (8, 128)) for k in range(2)]

    def both(step):
        for k in range(2):
            step(k)
        fence()

    fields = [[(Field(0, f0.at[k]), Field(0, a0.at[k]), Field(0, b0.at[k])) for k in range(2)],
              [(Field(1, f1.at[k]), Field(1, a1.at[k]), Field(1, b1.at[k])) for k in range(2)]]

    def small(f, lam):
        level = f.level
        if level == LEVELS - 1:
            return coarsest(f, lam, lanes)
        v, coarse = Field(level), Field(level + 1)
        first_two(f, v, lam, lanes)
        coarsen(v, f, coarse, lam, lanes)
        correct(v, small(coarse, lam))
        for _ in range(2):
            new = Field(level)
            sweep(v, f, new, lam, lanes)
            v = new
        return v

    def cycle(level, first):
        def parts(k):
            return fields[level][k]

        def named(name, step):
            with scope(f"{name}_{level}"):
                both(step)

        if first:
            named("first_two", lambda k: first_two(parts(k)[0], parts(k)[2], lams[k], lanes))
        else:
            named("sweep", lambda k: sweep(parts(k)[2], parts(k)[0], parts(k)[1], lams[k], lanes))
            named("sweep", lambda k: sweep(parts(k)[1], parts(k)[0], parts(k)[2], lams[k], lanes))
        if level == 0:
            named("coarsen", lambda k: coarsen(parts(k)[2], parts(k)[0], fields[1][k][0], lams[k], lanes))
            cycle(1, True)
            named("correct", lambda k: correct(parts(k)[2], fields[1][k][2]))
        else:
            def inner(k):
                coarse = Field(2)
                coarsen(parts(k)[2], parts(k)[0], coarse, lams[k], lanes)
                correct(parts(k)[2], small(coarse, lams[k]))

            named("inner", inner)
        named("sweep", lambda k: sweep(parts(k)[2], parts(k)[0], parts(k)[1], lams[k], lanes))
        named("sweep", lambda k: sweep(parts(k)[1], parts(k)[0], parts(k)[2], lams[k], lanes))

    cycle(0, True)
    cycle(0, False)

    with scope("repack"):
        for k in range(2):
            edge = w_ref.at[8 + k]
            for y in range(4):
                low = edge[pl.ds(y, 8, stride=4), :] + b0[k, BX - 1, y]
                high = edge[pl.ds(32 + y, 8, stride=4), :] + b0[k, 0, y]
                edge[pl.ds(y, 8, stride=4), :] = lanes.from_left(low)
                edge[pl.ds(32 + y, 8, stride=4), :] = lanes.from_right(high)
            for x in range(BX):
                edge[64 + x : 65 + x, :] = row_ref[k, x : x + 1] + lanes.from_below(b0[k, x, 3])[7:8]
                edge[80 + x : 81 + x, :] = row_ref[k, 16 + x : 17 + x] + lanes.from_above(b0[k, x, 0])[0:1]
                t, x4 = divmod(x, 4)
                for y in range(4):
                    w_ref[2 * t + k, pl.ds(32 * x4 + y, 8, stride=4), :] = b0[k, x, y]
        fence()
        for n in range(ROWS):
            reply[pl.ds(n, NDEV, stride=ROWS), :] = w_ref[n].T

    with scope("a2a_2_start"):
        start_all_to_all(reply, back, 1)
    with scope("a2a_2_wait"):
        wait_all(back, r_sem.at[1])

    with scope("idst"):
        for t in range(TILES):
            for k in range(2):
                o_ref[t, pl.ds(k, NDEV, stride=2), :] = back[pl.ds(2 * t + k, NDEV, stride=ROWS), :]
        for t in range(4):
            e_ref[4 * t : 4 * t + 4] = transform(o_ref[t], s_ref[...], 0).reshape(4, BY, NZ)
        ends_ref[...] = transform(o_ref[4], s_ref[...], 0)

    with scope("final"):
        for i in range(BX):
            e = e_ref[i]
            p = p_ref[i] + e
            pressure_ref[i] = p
            r = r_ref[i] - 4.0 * e + (shifted_depth(p, False) + shifted_depth(p, True) - 2.0 * p)
            r = r + (shifted_rows(e, False) + shifted_rows(e, True))
            r = r + (e_ref[i - 1] if i > 0 else ends_ref[0:32])
            r = r + (e_ref[i + 1] if i < BX - 1 else ends_ref[32:64])
            residual_ref[i] = r
            residual_ref[i, 0] = residual_ref[i, 0] + ends_ref[64 + i]
            residual_ref[i, BY - 1] = residual_ref[i, BY - 1] + ends_ref[80 + i]

    with scope("store"):
        stores = [
            pltpu.make_async_copy(source, target, out_sem.at[n])
            for n, (source, target) in enumerate(((pressure_ref, pressure_hbm), (residual_ref, residual_hbm)))
        ]
        for store in stores:
            store.start()
        wait_all(send, s_sem.at[0])
        wait_all(reply, s_sem.at[1])
        for store in stores:
            store.wait()


def on_device(forces, pressure_prev):
    block = (BX, BY, NZ)
    anywhere = pl.BlockSpec(memory_space=pl.ANY)

    def vmem(*shape):
        return pltpu.VMEM(shape, jnp.float32)

    return pl.pallas_call(
        kernel,
        out_shape=(jax.ShapeDtypeStruct(block, jnp.float32), jax.ShapeDtypeStruct(block, jnp.float32)),
        in_specs=[anywhere] * 5,
        out_specs=(anywhere, anywhere),
        scratch_shapes=[
            vmem(3, *block), vmem(*block), vmem(NZ, NZ), vmem(NZ, NZ), vmem(8, 128),
            vmem(*block), vmem(128, NZ), vmem(TILES, NZ, 128), vmem(*block), vmem(128, NZ), vmem(*block), vmem(*block),
            vmem(NDEV * ROWS, 128), vmem(NDEV * ROWS, 128), vmem(NDEV * ROWS, 128), vmem(NDEV * ROWS, 128),
            vmem(ROWS, 128, 128), vmem(2, 32, 128),
            *[vmem(2, 16, 4, 8, 128)] * 3, *[vmem(2, 8, 2, 8, 128)] * 3,
            pltpu.SemaphoreType.DMA((5,)),
            pltpu.SemaphoreType.DMA((2,)),
            pltpu.SemaphoreType.DMA((2,)),
            pltpu.SemaphoreType.DMA((2,)),
        ],
        compiler_params=pltpu.CompilerParams(collective_id=0, has_side_effects=True),
        name="poisson",
    )(
        forces,
        pressure_prev,
        jnp.asarray(sine_matrix()),
        jnp.asarray(sine_matrix(-spectrum()[:, None])),
        jnp.asarray(eigenvalues()),
    )


def solution(mesh):
    return jax.shard_map(
        on_device,
        mesh=mesh,
        in_specs=(P(None, "gx", "gy", None), P("gx", "gy", None)),
        out_specs=(P("gx", "gy", None), P("gx", "gy", None)),
        check_vma=False,
    )
```

time: 1490 us -> 46.4 us (0.03); the launches traced: 1460 us -> 46.2 us
  loops' own time: 875 us -> 0 us
  starting transfers between devices: 229 us -> 0 us
  between operations: 125 us -> 0.64 us
  waiting for transfers between devices: 112 us -> 0 us
  local copies, waits for them, and re-layouts: 85.8 us -> 3.76 us
  Pallas kernels: 0 us -> 41.8 us
  blocking collectives: 21.6 us -> 0 us
  other arithmetic: 16.8 us -> 0 us
    another operation x4 -> x0, loops' own time: 875 us -> none  [mean_mode(): lax.linalg.tridiagonal_solve(lower, middle, upper, column[:, None])[:, 0]]
    ppermute x102 -> x0, starting transfers between devices: 217 us -> none  [the longest x32 105 us: padded_2(): after = lax.ppermute(initial, axis, down)]
    ppermute x102 -> x0, waiting for transfers between devices: 97.3 us -> none  [the longest x32 38.6 us: padded_2(): before = lax.ppermute(last, axis, up)]
    slice x175 -> x0, local copies, waits for them, and re-layouts: 70.9 us -> none  [the longest x102 69.6 us: mean_mode(): lax.linalg.tridiagonal_solve(lower, middle, upper, column[:, None])[:, 0]]
    pallas_call x0 -> x1, Pallas kernels: none -> 41.8 us  [on_device(): pl.pallas_call(kernel, out_shape=(jax.ShapeDtypeStruct(block, jnp.float32...]
    all_to_all x2 -> x0, blocking collectives: 21.6 us -> none  [sent_to_all(): return lax.all_to_all(copies, axis, split_axis=0, concat_axis=0, tiled=True)]
  transfers between devices with their start and end apart: 104 -> 0, of which waited for: 72 -> 0; matrix products, arithmetic and copies ran while one was open for 0% -> 0% of each run, Pallas kernels for 0% -> 0%
where the time goes in v2:
time: 46.4 us; the launch traced here: 46.2 us
  Pallas kernels  41.8 us (90%)
  local copies, waits for them, and re-layouts  3.76 us (8%)
  between operations  0.64 us (1%)
    pallas_call x1, Pallas kernels, on_device(): pl.pallas_call(kernel, out_shape=(jax.ShapeDtypeStruct(block, jnp.float32...  41.8 us
    unnamed x2, local copies, waits for them, and re-layouts  3.76 us

profile of v2, /device:TPU:1, one launch (start us, length us, event | category | flops | bytes accessed | tf_op | source)
XLA Modules:
  0.0 46.2 jit_solution(18178965681929187142)
XLA Ops:
  0.6 41.8 %poisson.1 = (f32[16,32,256]{2,1,0:T(8,128)}, f32[16,32,256]{2,1,0:T(8,128)}) custom-call(f32[3,16,32,256]{3,2,1,0:T(8,128)} %f_hbm.1, f32[16,32,256]{2,1,0:T(8,128)} %p_hbm.1, f32[256,256]{1,0:T(8,128)} %constant.6.clone.s_hbm, f32[256,256]{1,0:T(8,128)} %constant.7.clone.st_hbm, f32[128,8,128]{2,1,0:T(8,128)} %constant.8.clone.lam_hbm), custom_call_target="tpu_custom_call" | custom-call | tf_op jit(solution)/shard_map/poisson/pallas_call | solution.py:420
  42.4 1.9 %copy.9 = f32[16,32,256]{2,1,0:T(8,128)} copy(f32[16,32,256]{2,1,0:T(8,128)} %get-tuple-element.4) | data formatting | bytes 1048576
  44.3 1.9 %copy.10 = f32[16,32,256]{2,1,0:T(8,128)} copy(f32[16,32,256]{2,1,0:T(8,128)} %get-tuple-element.5) | data formatting | bytes 1048576

commit v3 on v2

--- a/solution.py
+++ b/solution.py
@@ -16,7 +16,6 @@
 NDEV = GX * GY
 BX, BY, NZ = 16, 32, 256
 TILES = 5
-ROWS = 2 * TILES
 HIGHEST = lax.Precision.HIGHEST
 SCOPES = False
 
@@ -32,7 +31,8 @@
 
 def sine_matrix(weight=1.0):
     k = np.arange(1, NZ + 1, dtype=np.float64)
-    return (weight * (np.sqrt(2.0 / (NZ + 1)) * np.sin(np.pi * np.outer(k, k) / (NZ + 1)))).astype(np.float32)
+    full = weight * (np.sqrt(2.0 / (NZ + 1)) * np.sin(np.pi * np.outer(k, k) / (NZ + 1)))
+    return np.concatenate([full[0::2], full[1::2]]).astype(np.float32)
 
 
 def eigenvalues():
@@ -185,10 +185,10 @@
 
 def kernel(
     f_hbm, p_hbm, s_hbm, st_hbm, lam_hbm,
-    pressure_hbm, residual_hbm,
-    f_ref, p_ref, s_ref, st_ref, lam_ref, r_ref, g_ref, o_ref, e_ref, ends_ref, pressure_ref, residual_ref,
+    pressure_ref, residual_ref,
+    f_ref, p_ref, s_ref, st_ref, lam_ref, r_ref, g_ref, o_ref, e_ref,
     send, recv, reply, back, w_ref, row_ref, f0, a0, b0, f1, a1, b1,
-    in_sem, out_sem, s_sem, r_sem,
+    in_sem, s_sem, r_sem,
 ):
     gx, gy = lax.axis_index("gx"), lax.axis_index("gy")
     me = gy * GX + gx
@@ -245,66 +245,58 @@
             o_ref[t] = transform(s_ref[...], rows, 1) + transform(st_ref[...], flat, 1)
         o_ref[4] = transform(s_ref[...], g_ref[...], 1)
     with scope("pack"):
-        for t in range(TILES):
-            for k in range(2):
-                send[pl.ds(2 * t + k, NDEV, stride=ROWS), :] = o_ref[t, pl.ds(k, NDEV, stride=2), :]
+        for k in range(2):
+            for t in range(TILES):
+                send[k, pl.ds(t, NDEV, stride=TILES), :] = o_ref[t, k * NDEV : (k + 1) * NDEV]
 
     with scope("barrier"):
         pl.semaphore_wait(barrier, NDEV - 1)
 
-    def blocks(ref, index):
-        return ref.at[pl.ds(index * ROWS, ROWS)]
-
     def start_all_to_all(source, target, which):
-        mine = blocks(target, me)
+        mine = target.at[pl.ds(me * TILES, TILES)]
 
         def visit(x, y):
             pltpu.make_async_remote_copy(
-                blocks(source, y * GX + x), mine, s_sem.at[which], r_sem.at[which], device_id=(x, y), device_id_type=MESH
+                source.at[pl.ds((y * GX + x) * TILES, TILES)], mine, s_sem.at[which], r_sem.at[which],
+                device_id=(x, y), device_id_type=MESH,
             ).start()
 
         partners(visit)
-        target[pl.ds(me * ROWS, ROWS), :] = source[pl.ds(me * ROWS, ROWS), :]
+        target[pl.ds(me * TILES, TILES), :] = source[pl.ds(me * TILES, TILES), :]
 
     def wait_all(ref, sem):
-        most = ref.at[pl.ds(0, (NDEV - 1) * ROWS)]
+        most = ref.at[pl.ds(0, (NDEV - 1) * TILES)]
         pltpu.make_async_copy(most, most, sem).wait()
 
     with scope("a2a_1_start"):
-        start_all_to_all(send, recv, 0)
-    with scope("a2a_1_wait"):
-        wait_all(recv, r_sem.at[0])
+        for k in range(2):
+            start_all_to_all(send.at[k], recv.at[k], k)
 
     lanes = Lanes()
-    with scope("unpack"):
-        for n in range(ROWS):
-            w_ref[n] = recv[pl.ds(n, NDEV, stride=ROWS), :].T
-        for k in range(2):
-            for half in range(2):
-                at = 8 * half
-                row_ref[k, at : at + 8] = lanes.from_below(w_ref[8 + k, 64 + at : 72 + at])
-                row_ref[k, 16 + at : 24 + at] = lanes.from_above(w_ref[8 + k, 80 + at : 88 + at])
-        for k in range(2):
-            for x in range(BX):
-                t, x4 = divmod(x, 4)
-                for y in range(4):
-                    value = w_ref[2 * t + k, pl.ds(32 * x4 + y, 8, stride=4), :]
-                    if x == 0:
-                        value = value + lanes.from_left(w_ref[8 + k, pl.ds(y, 8, stride=4), :])
-                    if x == BX - 1:
-                        value = value + lanes.from_right(w_ref[8 + k, pl.ds(32 + y, 8, stride=4), :])
-                    if y == 0:
-                        value = value + jnp.where(lanes.sub == 0, row_ref[k, x : x + 1], 0.0)
-                    if y == 3:
-                        value = value + jnp.where(lanes.sub == 7, row_ref[k, 16 + x : 17 + x], 0.0)
-                    f0[k, x, y] = value
+
+    def unpack(k):
+        w = w_ref.at[k]
+        for n in range(TILES):
+            w[n] = recv[k, pl.ds(n, NDEV, stride=TILES), :].T
+        for half in range(2):
+            at = 8 * half
+            row_ref[k, at : at + 8] = lanes.from_below(w[4, 64 + at : 72 + at])
+            row_ref[k, 16 + at : 24 + at] = lanes.from_above(w[4, 80 + at : 88 + at])
+        for x in range(BX):
+            t, x4 = divmod(x, 4)
+            for y in range(4):
+                value = w[t, pl.ds(32 * x4 + y, 8, stride=4), :]
+                if x == 0:
+                    value = value + lanes.from_left(w[4, pl.ds(y, 8, stride=4), :])
+                if x == BX - 1:
+                    value = value + lanes.from_right(w[4, pl.ds(32 + y, 8, stride=4), :])
+                if y == 0:
+                    value = value + jnp.where(lanes.sub == 0, row_ref[k, x : x + 1], 0.0)
+                if y == 3:
+                    value = value + jnp.where(lanes.sub == 7, row_ref[k, 16 + x : 17 + x], 0.0)
+                f0[k, x, y] = value
 
     lams = [jnp.broadcast_to(lam_ref[k : k + 1], (8, 128)) for k in range(2)]
-
-    def both(step):
-        for k in range(2):
-            step(k)
-        fence()
 
     fields = [[(Field(0, f0.at[k]), Field(0, a0.at[k]), Field(0, b0.at[k])) for k in range(2)],
               [(Field(1, f1.at[k]), Field(1, a1.at[k]), Field(1, b1.at[k])) for k in range(2)]]
@@ -323,91 +315,94 @@
             v = new
         return v
 
-    def cycle(level, first):
-        def parts(k):
-            return fields[level][k]
-
-        def named(name, step):
+    def cycle(k, level, first):
+        f, a, b = fields[level][k]
+        lam = lams[k]
+
+        def named(name, step, *args):
             with scope(f"{name}_{level}"):
-                both(step)
+                step(*args, lam, lanes)
+            fence()
 
         if first:
-            named("first_two", lambda k: first_two(parts(k)[0], parts(k)[2], lams[k], lanes))
-        else:
-            named("sweep", lambda k: sweep(parts(k)[2], parts(k)[0], parts(k)[1], lams[k], lanes))
-            named("sweep", lambda k: sweep(parts(k)[1], parts(k)[0], parts(k)[2], lams[k], lanes))
+            named("first_two", first_two, f, b)
+        else:
+            named("sweep", sweep, b, f, a)
+            named("sweep", sweep, a, f, b)
         if level == 0:
-            named("coarsen", lambda k: coarsen(parts(k)[2], parts(k)[0], fields[1][k][0], lams[k], lanes))
-            cycle(1, True)
-            named("correct", lambda k: correct(parts(k)[2], fields[1][k][2]))
-        else:
-            def inner(k):
+            named("coarsen", coarsen, b, f, fields[1][k][0])
+            cycle(k, 1, True)
+            named("correct", lambda v, e, *_: correct(v, e), b, fields[1][k][2])
+        else:
+            def inner(*_):
                 coarse = Field(2)
-                coarsen(parts(k)[2], parts(k)[0], coarse, lams[k], lanes)
-                correct(parts(k)[2], small(coarse, lams[k]))
+                coarsen(b, f, coarse, lam, lanes)
+                correct(b, small(coarse, lam))
 
             named("inner", inner)
-        named("sweep", lambda k: sweep(parts(k)[2], parts(k)[0], parts(k)[1], lams[k], lanes))
-        named("sweep", lambda k: sweep(parts(k)[1], parts(k)[0], parts(k)[2], lams[k], lanes))
-
-    cycle(0, True)
-    cycle(0, False)
-
-    with scope("repack"):
-        for k in range(2):
-            edge = w_ref.at[8 + k]
+        named("sweep", sweep, b, f, a)
+        named("sweep", sweep, a, f, b)
+
+    def repack(k):
+        w = w_ref.at[k]
+        edge = w.at[4]
+        for y in range(4):
+            low = edge[pl.ds(y, 8, stride=4), :] + b0[k, BX - 1, y]
+            high = edge[pl.ds(32 + y, 8, stride=4), :] + b0[k, 0, y]
+            edge[pl.ds(y, 8, stride=4), :] = lanes.from_left(low)
+            edge[pl.ds(32 + y, 8, stride=4), :] = lanes.from_right(high)
+        for x in range(BX):
+            edge[64 + x : 65 + x, :] = row_ref[k, x : x + 1] + lanes.from_below(b0[k, x, 3])[7:8]
+            edge[80 + x : 81 + x, :] = row_ref[k, 16 + x : 17 + x] + lanes.from_above(b0[k, x, 0])[0:1]
+            t, x4 = divmod(x, 4)
             for y in range(4):
-                low = edge[pl.ds(y, 8, stride=4), :] + b0[k, BX - 1, y]
-                high = edge[pl.ds(32 + y, 8, stride=4), :] + b0[k, 0, y]
-                edge[pl.ds(y, 8, stride=4), :] = lanes.from_left(low)
-                edge[pl.ds(32 + y, 8, stride=4), :] = lanes.from_right(high)
-            for x in range(BX):
-                edge[64 + x : 65 + x, :] = row_ref[k, x : x + 1] + lanes.from_below(b0[k, x, 3])[7:8]
-                edge[80 + x : 81 + x, :] = row_ref[k, 16 + x : 17 + x] + lanes.from_above(b0[k, x, 0])[0:1]
-                t, x4 = divmod(x, 4)
-                for y in range(4):
-                    w_ref[2 * t + k, pl.ds(32 * x4 + y, 8, stride=4), :] = b0[k, x, y]
+                w[t, pl.ds(32 * x4 + y, 8, stride=4), :] = b0[k, x, y]
         fence()
-        for n in range(ROWS):
-            reply[pl.ds(n, NDEV, stride=ROWS), :] = w_ref[n].T
-
-    with scope("a2a_2_start"):
-        start_all_to_all(reply, back, 1)
-    with scope("a2a_2_wait"):
-        wait_all(back, r_sem.at[1])
-
-    with scope("idst"):
-        for t in range(TILES):
-            for k in range(2):
-                o_ref[t, pl.ds(k, NDEV, stride=2), :] = back[pl.ds(2 * t + k, NDEV, stride=ROWS), :]
-        for t in range(4):
-            e_ref[4 * t : 4 * t + 4] = transform(o_ref[t], s_ref[...], 0).reshape(4, BY, NZ)
-        ends_ref[...] = transform(o_ref[4], s_ref[...], 0)
+        for n in range(TILES):
+            reply[k, pl.ds(n, NDEV, stride=TILES), :] = w[n].T
+
+    for k in range(2):
+        with scope(f"a2a_1_wait_{k}"):
+            wait_all(recv.at[k], r_sem.at[k])
+        with scope("unpack"):
+            unpack(k)
+        fence()
+        cycle(k, 0, True)
+        cycle(k, 0, False)
+        with scope("repack"):
+            repack(k)
+        with scope("a2a_2_start"):
+            start_all_to_all(reply.at[k], back.at[k], 2 + k)
+
+    for k in range(2):
+        with scope(f"a2a_2_wait_{k}"):
+            wait_all(back.at[k], r_sem.at[2 + k])
+        with scope("idst"):
+            basis = s_ref[k * NDEV : (k + 1) * NDEV]
+            for t in range(TILES):
+                part = transform(back[k, pl.ds(t, NDEV, stride=TILES), :], basis, 0)
+                e_ref[t] = part if k == 0 else e_ref[t] + part
+
+    def plane(i):
+        return e_ref[i // 4, 32 * (i % 4) : 32 * (i % 4) + 32]
 
     with scope("final"):
         for i in range(BX):
-            e = e_ref[i]
+            e = plane(i)
             p = p_ref[i] + e
             pressure_ref[i] = p
             r = r_ref[i] - 4.0 * e + (shifted_depth(p, False) + shifted_depth(p, True) - 2.0 * p)
             r = r + (shifted_rows(e, False) + shifted_rows(e, True))
-            r = r + (e_ref[i - 1] if i > 0 else ends_ref[0:32])
-            r = r + (e_ref[i + 1] if i < BX - 1 else ends_ref[32:64])
+            r = r + (plane(i - 1) if i > 0 else e_ref[4, 0:32])
+            r = r + (plane(i + 1) if i < BX - 1 else e_ref[4, 32:64])
             residual_ref[i] = r
-            residual_ref[i, 0] = residual_ref[i, 0] + ends_ref[64 + i]
-            residual_ref[i, BY - 1] = residual_ref[i, BY - 1] + ends_ref[80 + i]
-
-    with scope("store"):
-        stores = [
-            pltpu.make_async_copy(source, target, out_sem.at[n])
-            for n, (source, target) in enumerate(((pressure_ref, pressure_hbm), (residual_ref, residual_hbm)))
-        ]
-        for store in stores:
-            store.start()
-        wait_all(send, s_sem.at[0])
-        wait_all(reply, s_sem.at[1])
-        for store in stores:
-            store.wait()
+            residual_ref[i, 0] = residual_ref[i, 0] + e_ref[4, 64 + i]
+            residual_ref[i, BY - 1] = residual_ref[i, BY - 1] + e_ref[4, 80 + i]
+
+    with scope("drain"):
+        for k in range(2):
+            wait_all(send.at[k], s_sem.at[k])
+            wait_all(reply.at[k], s_sem.at[2 + k])
 
 
 def on_device(forces, pressure_prev):
@@ -419,19 +414,17 @@
 
     return pl.pallas_call(
         kernel,
-        out_shape=(jax.ShapeDtypeStruct(block, jnp.float32), jax.ShapeDtypeStruct(block, jnp.float32)),
+        out_shape=(pltpu.VMEM(block, jnp.float32), pltpu.VMEM(block, jnp.float32)),
         in_specs=[anywhere] * 5,
-        out_specs=(anywhere, anywhere),
+        out_specs=(pl.BlockSpec(memory_space=pltpu.VMEM),) * 2,
         scratch_shapes=[
             vmem(3, *block), vmem(*block), vmem(NZ, NZ), vmem(NZ, NZ), vmem(8, 128),
-            vmem(*block), vmem(128, NZ), vmem(TILES, NZ, 128), vmem(*block), vmem(128, NZ), vmem(*block), vmem(*block),
-            vmem(NDEV * ROWS, 128), vmem(NDEV * ROWS, 128), vmem(NDEV * ROWS, 128), vmem(NDEV * ROWS, 128),
-            vmem(ROWS, 128, 128), vmem(2, 32, 128),
+            vmem(*block), vmem(128, NZ), vmem(TILES, NZ, 128), vmem(TILES, 128, NZ),
+            *[vmem(2, NDEV * TILES, 128)] * 4, vmem(2, TILES, 128, 128), vmem(2, 32, 128),
             *[vmem(2, 16, 4, 8, 128)] * 3, *[vmem(2, 8, 2, 8, 128)] * 3,
             pltpu.SemaphoreType.DMA((5,)),
-            pltpu.SemaphoreType.DMA((2,)),
-            pltpu.SemaphoreType.DMA((2,)),
-            pltpu.SemaphoreType.DMA((2,)),
+            pltpu.SemaphoreType.DMA((4,)),
+            pltpu.SemaphoreType.DMA((4,)),
         ],
         compiler_params=pltpu.CompilerParams(collective_id=0, has_side_effects=True),
         name="poisson",

time: 46.4 us -> 41.4 us (0.89)
  Pallas kernels: 41.8 us -> 39 us
  local copies, waits for them, and re-layouts: 3.76 us -> 1.59 us
    pallas_call x1, Pallas kernels: 41.8 us -> 39 us  [on_device(): pl.pallas_call(kernel, out_shape=(pltpu.VMEM(block, jnp.float32), pltpu.V...]
    unnamed x2, local copies, waits for them, and re-layouts: 3.76 us -> 1.59 us
where the time goes in v3:
time: 41.4 us; the launch traced here: 41.2 us
  Pallas kernels  39 us (94%)
  local copies, waits for them, and re-layouts  1.59 us (4%)
  between operations  0.64 us (2%)
    pallas_call x1, Pallas kernels, on_device(): pl.pallas_call(kernel, out_shape=(pltpu.VMEM(block, jnp.float32), pltpu.V...  39 us
    unnamed x2, local copies, waits for them, and re-layouts  1.59 us

profile of v3, /device:TPU:1, one launch (start us, length us, event | category | flops | bytes accessed | tf_op | source)
XLA Modules:
  0.0 41.2 jit_solution(5352368428496615570)
XLA Ops:
  0.6 39.0 %poisson.1 = (f32[16,32,256]{2,1,0:T(8,128)S(1)}, f32[16,32,256]{2,1,0:T(8,128)S(1)}) custom-call(f32[3,16,32,256]{3,2,1,0:T(8,128)} %f_hbm.1, f32[16,32,256]{2,1,0:T(8,128)} %p_hbm.1, f32[256,256]{1,0:T(8,128)} %constant.6.clone.s_hbm, f32[256,256]{1,0:T(8,128)} %constant.7.clone.st_hbm, f32[128,8,128]{2,1,0:T(8,128)} %constant.8.clone.lam_hbm), custom_call_target="tpu_custom_call" | custom-call | tf_op jit(solution)/shard_map/poisson/pallas_call | solution.py:415
  39.7 0.8 %copy.9 = f32[16,32,256]{2,1,0:T(8,128)} copy(f32[16,32,256]{2,1,0:T(8,128)S(1)} %get-tuple-element.2) | data formatting | bytes 1048576
  40.5 0.8 %copy.10 = f32[16,32,256]{2,1,0:T(8,128)} copy(f32[16,32,256]{2,1,0:T(8,128)S(1)} %get-tuple-element.3) | data formatting | bytes 1048576
